TPU v7x, 128 devices: a whole 4x4x4 slice. The times are simulated.
128 devices in a mesh: section: 4 (over z), dp: 8 (over y, core), mp: 4 (over x).
Axes of the slice: x: 4, y: 4, z: 4, core: 2. Of those that a mesh axis runs over, the one named last changes fastest.
Arguments:
- text: bfloat16 [4, 4096, 4096], P('section', ('dp', 'mp')), may hold values from -6 to 6
- patches: bfloat16 [16384, 1024], P(('section', 'dp')), may hold values from -6 to 6
- segments: int32 [4, 8, 512], P('section', 'dp'), may hold values from 0 to 3, never falling along the last dimension, each value on 1 to 256 neighbouring positions
- loss_mask: int32 [4, 4096], P('section', ('dp', 'mp')), may hold values from 0 to 1, as said below
- tile_batch: int32 [8, 8], P('dp'), may hold values from 0 to 3, as said below
- tile_offset: int32 [8, 8], P('dp'), may hold values from 0 to 448, as said below
- attn_gain: float32 [4, 4096], P('section'), may hold values from 0.5 to 2
- w_query: bfloat16 [4, 4096, 2048], P('section', None, 'mp'), may hold values from -0.09375 to 0.09375
- w_kv: bfloat16 [4, 2, 4096, 512], P('section', None, None, 'mp'), may hold values from -0.09375 to 0.09375
- w_out: bfloat16 [4, 2048, 4096], P('section', 'mp'), may hold values from -0.125 to 0.125
- vis_gain: float32 [2, 1024], replicated, may hold values from 0.5 to 2
- vis_bias: float32 [2, 1024], replicated, may hold values from -3 to 3
- v_qkv: bfloat16 [3, 1024, 1024], P(None, ('section', 'dp'), 'mp'), may hold values from -0.1875 to 0.1875
- v_out: bfloat16 [1024, 1024], P('mp', ('section', 'dp')), may hold values from -0.1875 to 0.1875
- v_up: bfloat16 [1024, 4096], P(('section', 'dp'), 'mp'), may hold values from -0.1875 to 0.1875
- v_down: bfloat16 [4096, 1024], P('mp', ('section', 'dp')), may hold values from -0.09375 to 0.09375
- v_proj: bfloat16 [4096, 4096], P(('section', 'dp'), 'mp'), may hold values from -0.09375 to 0.09375
Outputs:
- hidden: bfloat16 [4, 4096, 4096], P('section', ('dp', 'mp'))
- token_weight: float32 [4, 4096], P('section', ('dp', 'mp'))
Inputs may be any that keep to these rules, and one draw needn't show every extreme that they name: `tile_batch`: in every data-parallel index, the 2 tiles of each section index go 1 to each of two different micro-batches; one micro-batch receives 1 tiles from every section index. `tile_offset`: offsets are multiples of 64; the runs of one sequence never intersect. `loss_mask`: the first position of every sequence is a one.
All inputs are finite; a program needn't handle non-finite values.
Results may differ from a plain program's by a relative error of at most 0.025.
Values may be sent and summed in bfloat16 or wider, within the bound.
A program may use at most 192 MiB of HBM per device.

v0:
```python
import jax
import jax.numpy as jnp
from jax import lax
from jax.sharding import Mesh
from jax.sharding import PartitionSpec as P

HD = 128
VHD = 64
GRID = 16
PATCH = 256
POOL = 64
SECTION_DP = ("section", "dp_0", "dp_1")
SECTION_DP_MP = ("section", "dp_0", "dp_1", "mp")
DP = ("dp_0", "dp_1")
DP_MP = ("dp_0", "dp_1", "mp")
EPS = 1e-05
ROPE_BASE = 500000.0
BLOCKED = -1e30


def copy_for_each(array, axis):
    copies = jnp.broadcast_to(array, (lax.axis_size(axis), *array.shape))
    return lax.all_to_all(copies, axis, split_axis=0, concat_axis=0, tiled=True)


def over_copies(array, axis):
    everything = copy_for_each(array, axis)
    return jnp.sum(everything.astype(jnp.float32), axis=0)


def laid_out(tiles, dim):
    lengths = list(tiles.shape[1:])
    lengths[dim] *= tiles.shape[0]
    return jnp.moveaxis(tiles, 0, dim).reshape(lengths)


def one_gather(arrays, axis, dims):
    flat = jnp.concatenate([a.reshape(-1) for a in arrays])
    lines, at, done = (lax.all_gather(flat, axis), 0, [])
    for a, dim in zip(arrays, dims):
        tiles = lines[:, at : at + a.size].reshape(-1, *a.shape)
        done.append(laid_out(tiles, dim))
        at += a.size
    return tuple(done)


def shifted(value, axis, steps):
    count = lax.axis_size(axis)
    pairs = [(source, (source + steps) % count) for source in range(count)]
    return lax.ppermute(value, axis, pairs)


def over_axes(array, axes):
    for axis in axes:
        array = lax.psum(array, axis)
    return array


def layer_norm(values, gain, bias):
    wide = values.astype(jnp.float32)
    center = wide - jnp.mean(wide, axis=-1, keepdims=True)
    spread = jnp.mean(center * center, axis=-1, keepdims=True)
    return (center * lax.rsqrt(spread + EPS) * gain + bias).astype(jnp.bfloat16)


def rms_norm(values, gain):
    wide = values.astype(jnp.float32)
    power = jnp.mean(wide * wide, axis=-1, keepdims=True)
    return (wide * lax.rsqrt(power + EPS) * gain).astype(jnp.bfloat16)


def rotate(values, positions):
    half_width = values.shape[-1] // 2
    freqs = ROPE_BASE ** (-2.0 * jnp.arange(half_width, dtype=jnp.float32) / values.shape[-1])
    angles = positions.astype(jnp.float32)[:, None] * freqs[None, :]
    cosine = jnp.cos(angles)[:, None, :]
    sinus_part = jnp.sin(angles)[:, None, :]
    first_half = values[..., :half_width]
    second_half = values[..., half_width:]
    return jnp.concatenate(
        [
            first_half * cosine - second_half * sinus_part,
            second_half * cosine + first_half * sinus_part,
        ],
        axis=-1,
    )


def pixel_shuffle(states):
    tile_count = states.shape[0] // PATCH
    side_half = GRID // 2
    width = states.shape[1]
    arranged = states.reshape(tile_count, side_half, 2, side_half, 2, width)
    return arranged.transpose(0, 1, 3, 2, 4, 5).reshape(
        tile_count * side_half * side_half, 4 * width
    )


def block_sum(partial_value):
    return over_copies(partial_value.astype(jnp.bfloat16), "mp").astype(jnp.float32)


def encode_tiles(patches, vis_gain, vis_bias, qkv_full, out_full, up_full, down_full, proj_full):
    tile_count = patches.shape[0] // PATCH
    local_width = qkv_full.shape[2]
    head_count = local_width // VHD
    normed = layer_norm(patches, vis_gain[0], vis_bias[0])
    projected = [
        jnp.dot(normed, qkv_full[index], preferred_element_type=jnp.float32)
        .astype(jnp.bfloat16)
        .reshape(tile_count, PATCH, head_count, VHD)
        for index in range(3)
    ]
    scores = jnp.einsum(
        "tqhd,tkhd->thqk", projected[0], projected[1], preferred_element_type=jnp.float32
    ) * VHD ** (-0.5)
    probs = jax.nn.softmax(scores, axis=-1).astype(jnp.bfloat16)
    mixed = (
        jnp.einsum("thqk,tkhd->tqhd", probs, projected[2], preferred_element_type=jnp.float32)
        .astype(jnp.bfloat16)
        .reshape(tile_count * PATCH, local_width)
    )
    attended = block_sum(jnp.dot(mixed, out_full, preferred_element_type=jnp.float32))
    residual = (patches.astype(jnp.float32) + attended).astype(jnp.bfloat16)
    normed_two = layer_norm(residual, vis_gain[1], vis_bias[1])
    inner = jax.nn.gelu(
        jnp.dot(normed_two, up_full, preferred_element_type=jnp.float32), approximate=False
    ).astype(jnp.bfloat16)
    fed = block_sum(jnp.dot(inner, down_full, preferred_element_type=jnp.float32))
    states = (residual.astype(jnp.float32) + fed).astype(jnp.bfloat16)
    return jnp.dot(pixel_shuffle(states), proj_full, preferred_element_type=jnp.float32).astype(
        jnp.bfloat16
    )


def decoder_layer(active, state, segment_ids, gain, w_query, w_kv, w_out):
    normed = rms_norm(state, gain)
    query_width = w_query.shape[1]
    pair_width = w_kv.shape[2]
    joined_width = query_width + 2 * pair_width
    model_width = w_out.shape[1]
    piece = lax.all_gather(normed, "mp", axis=0, tiled=True)
    row_count = piece.shape[0]

    def project_computed(rows):
        positions = jnp.arange(row_count, dtype=jnp.int32)
        query = jnp.dot(rows, w_query, preferred_element_type=jnp.float32).reshape(
            row_count, query_width // HD, HD
        )
        keyed = jnp.dot(rows, w_kv[0], preferred_element_type=jnp.float32).reshape(
            row_count, pair_width // HD, HD
        )
        valued = jnp.dot(rows, w_kv[1], preferred_element_type=jnp.float32)
        return jnp.concatenate(
            [
                rotate(query, positions).reshape(row_count, query_width),
                rotate(keyed, positions).reshape(row_count, pair_width),
                valued,
            ],
            axis=1,
        ).astype(jnp.bfloat16)

    def project_skipped(rows):
        return jnp.zeros((row_count, joined_width), jnp.bfloat16)

    joined = lax.cond(active, project_computed, project_skipped, piece)
    length = joined.shape[0]
    pair_heads = pair_width // HD
    group_size = query_width // pair_width

    def attend(joined_rows):
        query = joined_rows[:, :query_width].reshape(length, pair_heads, group_size, HD)
        keyed = joined_rows[:, query_width : query_width + pair_width].reshape(
            length, pair_heads, HD
        )
        valued = joined_rows[:, query_width + pair_width :].reshape(length, pair_heads, HD)
        scores = jnp.einsum(
            "qkgd,skd->kgqs", query, keyed, preferred_element_type=jnp.float32
        ) * HD ** (-0.5)
        row_ids = jnp.arange(length, dtype=jnp.int32)
        allowed = (segment_ids[:, None] == segment_ids[None, :]) & (
            row_ids[None, :] <= row_ids[:, None]
        )
        scores = jnp.where(allowed, scores, BLOCKED)
        probs = jax.nn.softmax(scores, axis=-1).astype(jnp.bfloat16)
        return (
            jnp.einsum("kgqs,skd->qkgd", probs, valued, preferred_element_type=jnp.float32)
            .astype(jnp.bfloat16)
            .reshape(length, query_width)
        )

    def attend_skipped(joined_rows):
        return jnp.zeros((length, query_width), jnp.bfloat16)

    mixed = lax.cond(active, attend, attend_skipped, joined)
    count = state.shape[0] * lax.axis_size("mp")

    def out_computed(values):
        return jnp.dot(values, w_out, preferred_element_type=jnp.float32)

    def out_skipped(values):
        return jnp.zeros((count, model_width), jnp.float32)

    summed = lax.psum_scatter(
        lax.cond(active, out_computed, out_skipped, mixed).astype(jnp.bfloat16),
        "mp",
        scatter_dimension=0,
        tiled=True,
    ).astype(jnp.float32)
    updated = (state.astype(jnp.float32) + summed).astype(jnp.bfloat16)
    return jnp.where(active, updated, state)


def shards(
    text,
    patches,
    segments,
    loss_mask,
    tile_batch,
    tile_offset,
    attn_gain,
    w_query,
    w_kv,
    w_out,
    vis_gain,
    vis_bias,
    v_qkv,
    v_out,
    v_up,
    v_down,
    v_proj,
):
    sections = lax.axis_size("section")
    section_at = lax.axis_index("section")
    part_at = lax.axis_index("mp")
    qkv_full, out_full, up_full, down_full, proj_full = one_gather(
        (v_qkv, v_out, v_up, v_down, v_proj), SECTION_DP, (1, 1, 0, 1, 0)
    )
    embedded = encode_tiles(
        patches, vis_gain, vis_bias, qkv_full, out_full, up_full, down_full, proj_full
    )
    length = segments.shape[2]
    tiles_here = embedded.shape[0] // POOL
    batch_all = tile_batch[0]
    offset_all = tile_offset[0]
    own_batch = lax.dynamic_slice_in_dim(batch_all, section_at * tiles_here, tiles_here, 0)
    capacity = tiles_here // 2
    block_rows = capacity * POOL
    local_ids = jnp.arange(tiles_here, dtype=jnp.int32)
    local_same = (own_batch[:, None] == own_batch[None, :]) & (
        local_ids[None, :] < local_ids[:, None]
    )
    local_rank = jnp.sum(local_same.astype(jnp.int32), axis=1)
    send_rows = jnp.arange(sections * block_rows, dtype=jnp.int32)
    send_target = send_rows // block_rows
    send_rank = send_rows % block_rows // POOL
    send_match = (own_batch[None, :] == send_target[:, None]) & (
        local_rank[None, :] == send_rank[:, None]
    )
    own_rows = jnp.arange(tiles_here * POOL, dtype=jnp.int32)
    send_pick = jnp.repeat(send_match, POOL, axis=1) & (
        (own_rows % POOL)[None, :] == (send_rows % POOL)[:, None]
    )
    blocks = jnp.dot(
        send_pick.astype(jnp.bfloat16), embedded, preferred_element_type=jnp.float32
    ).astype(jnp.bfloat16)
    arrived = lax.all_to_all(blocks, "section", split_axis=0, concat_axis=0, tiled=True)
    tile_ids = jnp.arange(batch_all.shape[0], dtype=jnp.int32)
    source_ids = tile_ids // tiles_here
    tile_same = (
        (batch_all[:, None] == batch_all[None, :])
        & (source_ids[:, None] == source_ids[None, :])
        & (tile_ids[None, :] < tile_ids[:, None])
    )
    tile_rank = jnp.sum(tile_same.astype(jnp.int32), axis=1)
    slot_rows = jnp.arange(sections * block_rows, dtype=jnp.int32)
    slot_source = slot_rows // block_rows
    slot_rank = slot_rows % block_rows // POOL
    match = (
        (batch_all[None, :] == section_at)
        & (source_ids[None, :] == slot_source[:, None])
        & (tile_rank[None, :] == slot_rank[:, None])
    )
    slot_place = jnp.sum(match.astype(jnp.int32) * offset_all[None, :], axis=1) + slot_rows % POOL
    slot_valid = jnp.any(match, axis=1)
    places = jnp.arange(length, dtype=jnp.int32)
    picker = ((places[:, None] == slot_place[None, :]) & slot_valid[None, :]).astype(jnp.bfloat16)
    image_cols = jnp.dot(picker, arrived, preferred_element_type=jnp.float32).astype(jnp.bfloat16)
    image_rows = lax.all_to_all(image_cols, "mp", split_axis=0, concat_axis=1, tiled=True)
    shard_rows = image_rows.shape[0]
    positions = part_at * shard_rows + jnp.arange(shard_rows, dtype=jnp.int32)
    covered = jnp.any(
        (batch_all[None, :] == section_at)
        & (positions[:, None] >= offset_all[None, :])
        & (positions[:, None] < offset_all[None, :] + POOL),
        axis=1,
    )
    start_state = jnp.where(covered[:, None], image_rows, text[0])
    gain_here = attn_gain[0]
    query_here = w_query[0]
    pair_here = w_kv[0]
    out_here = w_out[0]
    state = start_state
    segment_ids = segments[0, 0]
    for tick_index in range(2 * sections):
        if tick_index < 2 * sections - 1:
            micro_at = jnp.mod(section_at - tick_index, sections)
            begin_at = jnp.mod(sections - micro_at, sections)
            active = (tick_index >= begin_at) & (tick_index < begin_at + sections)
            state = decoder_layer(
                active, state, segment_ids, gain_here, query_here, pair_here, out_here
            )
        state, segment_ids = shifted((state, segment_ids), "section", 1)
    totals = over_axes(jnp.sum(loss_mask), SECTION_DP_MP)
    scaling = float(sections * lax.axis_size(DP) * length)
    token_weight = loss_mask.astype(jnp.float32) * scaling / totals.astype(jnp.float32)
    return (state[None], token_weight)


def solution(mesh):
    split = Mesh(
        mesh.devices.reshape(mesh.shape["section"], 4, 2, mesh.shape["mp"]),
        ("section", "dp_0", "dp_1", "mp"),
    )
    return jax.shard_map(
        shards,
        mesh=split,
        in_specs=(
            P("section", DP_MP, None),
            P(SECTION_DP, None),
            P("section", DP, None),
            P("section", DP_MP),
            P(DP, None),
            P(DP, None),
            P("section", None),
            P("section", None, "mp"),
            P("section", None, None, "mp"),
            P("section", "mp", None),
            P(),
            P(),
            P(None, SECTION_DP, "mp"),
            P("mp", SECTION_DP),
            P(SECTION_DP, "mp"),
            P("mp", SECTION_DP),
            P(SECTION_DP, "mp"),
        ),
        out_specs=(P("section", DP_MP, None), P("section", DP_MP)),
        check_vma=False,
    )
```

profile of v0, /device:TPU:32, one launch (start us, length us, event | category | flops | bytes accessed | tf_op | source)
XLA Modules:
  0.0 1387.6 jit_solution(4361427265575410445)
XLA Ops:
  16.4 66.2 %all-gather.24.cloned.1.call-done = bf16[7340032]{0:T(1024)(128)(2,1)} async-done(((bf16[229376]{0:T(1024)(128)(2,1)}), bf16[7340032]{0:T(1024)(128)(2,1)}) %all-gather.24.cloned.1.call-update) | async-done | bytes 14680080 | tf_op jit(solution)/shard_map/all_gather | solution.py:39
  82.6 13.2 reshape.1320
  141.0 27.2 %all-to-all-done = bf16[4,512,1024]{2,1,0:T(8,128)(2,1)} async-done(((bf16[4,512,1024]{2,1,0:T(8,128)(2,1)}), bf16[4,512,1024]{2,1,0:T(8,128)(2,1)}, u32[]{:S(2)}, u32[]{:S(2)}) %all-to-all-start) | async-done | bytes 4194336 | tf_op jit(solution)/shard_map/all_to_all | solution.py:23
  205.8 31.9 %all-to-all-done.1 = bf16[4,512,1024]{2,1,0:T(8,128)(2,1)} async-done(((bf16[4,512,1024]{2,1,0:T(8,128)(2,1)}), bf16[4,512,1024]{2,1,0:T(8,128)(2,1)}, u32[]{:S(2)}, u32[]{:S(2)}) %all-to-all-start.1) | async-done | bytes 4194336 | tf_op jit(solution)/shard_map/all_to_all | solution.py:23
  268.5 11.0 all-to-all-done.3
  285.6 46.9 %all-gather.10.cloned.1.call-done = bf16[512,4096]{1,0:T(8,128)(2,1)} async-done(((bf16[128,4096]{1,0:T(8,128)(2,1)}), bf16[512,4096]{1,0:T(8,128)(2,1)}) %all-gather.10.cloned.1.call-update) | async-done | bytes 4194320 | tf_op jit(solution)/shard_map/all_gather | solution.py:142
  341.9 62.8 %reduce-scatter.8.cloned.1.call-done = bf16[128,4096]{1,0:T(8,128)(2,1)} async-done(((bf16[512,4096]{1,0:T(8,128)(2,1)}), bf16[128,4096]{1,0:T(8,128)(2,1)}) %reduce-scatter.8.cloned.1.call-update) | async-done | bytes 1048592 | tf_op jit(solution)/shard_map/reduce_scatter | solution.py:204
  408.5 23.3 %collective-permute-done = bf16[128,4096]{1,0:T(8,128)(2,1)S(1)} collective-permute-done((bf16[128,4096]{1,0:T(8,128)(2,1)S(1)}, bf16[128,4096]{1,0:T(8,128)(2,1)S(1)}, u32[]{:S(2)}, u32[]{:S(2)}) %collective-permute-start) | collective-permute-done | bytes 1048608 | tf_op jit(solution)/shard_map/ppermute | solution.py:50
  435.0 46.4 %all-gather.12.cloned.1.call-done = bf16[512,4096]{1,0:T(8,128)(2,1)} async-done(((bf16[128,4096]{1,0:T(8,128)(2,1)}), bf16[512,4096]{1,0:T(8,128)(2,1)}) %all-gather.12.cloned.1.call-update) | async-done | bytes 4194320 | tf_op jit(solution)/shard_map/all_gather | solution.py:142
  491.6 10.4 conditional.25
  509.2 45.7 %reduce-scatter.10.cloned.1.call-done = bf16[128,4096]{1,0:T(8,128)(2,1)} async-done(((bf16[512,4096]{1,0:T(8,128)(2,1)}), bf16[128,4096]{1,0:T(8,128)(2,1)}) %reduce-scatter.10.cloned.1.call-update) | async-done | bytes 1048592 | tf_op jit(solution)/shard_map/reduce_scatter | solution.py:204
  558.0 23.3 %collective-permute-done.2 = bf16[128,4096]{1,0:T(8,128)(2,1)S(1)} collective-permute-done((bf16[128,4096]{1,0:T(8,128)(2,1)S(1)}, bf16[128,4096]{1,0:T(8,128)(2,1)S(1)}, u32[]{:S(2)}, u32[]{:S(2)}) %collective-permute-start.2) | collective-permute-done | bytes 1048608 | tf_op jit(solution)/shard_map/ppermute | solution.py:50
  584.6 46.4 %all-gather.14.cloned.1.call-done = bf16[512,4096]{1,0:T(8,128)(2,1)} async-done(((bf16[128,4096]{1,0:T(8,128)(2,1)}), bf16[512,4096]{1,0:T(8,128)(2,1)}) %all-gather.14.cloned.1.call-update) | async-done | bytes 4194320 | tf_op jit(solution)/shard_map/all_gather | solution.py:142
  641.2 10.6 conditional.28
  658.6 47.3 %reduce-scatter.12.cloned.1.call-done = bf16[128,4096]{1,0:T(8,128)(2,1)} async-done(((bf16[512,4096]{1,0:T(8,128)(2,1)}), bf16[128,4096]{1,0:T(8,128)(2,1)}) %reduce-scatter.12.cloned.1.call-update) | async-done | bytes 1048592 | tf_op jit(solution)/shard_map/reduce_scatter | solution.py:204
  709.0 23.3 %collective-permute-done.4 = bf16[128,4096]{1,0:T(8,128)(2,1)S(1)} collective-permute-done((bf16[128,4096]{1,0:T(8,128)(2,1)S(1)}, bf16[128,4096]{1,0:T(8,128)(2,1)S(1)}, u32[]{:S(2)}, u32[]{:S(2)}) %collective-permute-start.4) | collective-permute-done | bytes 1048608 | tf_op jit(solution)/shard_map/ppermute | solution.py:50
  735.6 46.4 %all-gather.16.cloned.1.call-done = bf16[512,4096]{1,0:T(8,128)(2,1)} async-done(((bf16[128,4096]{1,0:T(8,128)(2,1)}), bf16[512,4096]{1,0:T(8,128)(2,1)}) %all-gather.16.cloned.1.call-update) | async-done | bytes 4194320 | tf_op jit(solution)/shard_map/all_gather | solution.py:142
  782.0 10.4 conditional.30
  792.3 10.5 conditional.31
  810.0 46.8 %reduce-scatter.14.cloned.1.call-done = bf16[128,4096]{1,0:T(8,128)(2,1)} async-done(((bf16[512,4096]{1,0:T(8,128)(2,1)}), bf16[128,4096]{1,0:T(8,128)(2,1)}) %reduce-scatter.14.cloned.1.call-update) | async-done | bytes 1048592 | tf_op jit(solution)/shard_map/reduce_scatter | solution.py:204
  860.0 23.3 %collective-permute-done.6 = bf16[128,4096]{1,0:T(8,128)(2,1)S(1)} collective-permute-done((bf16[128,4096]{1,0:T(8,128)(2,1)S(1)}, bf16[128,4096]{1,0:T(8,128)(2,1)S(1)}, u32[]{:S(2)}, u32[]{:S(2)}) %collective-permute-start.6) | collective-permute-done | bytes 1048608 | tf_op jit(solution)/shard_map/ppermute | solution.py:50
  886.6 46.4 %all-gather.18.cloned.1.call-done = bf16[512,4096]{1,0:T(8,128)(2,1)} async-done(((bf16[128,4096]{1,0:T(8,128)(2,1)}), bf16[512,4096]{1,0:T(8,128)(2,1)}) %all-gather.18.cloned.1.call-update) | async-done | bytes 4194320 | tf_op jit(solution)/shard_map/all_gather | solution.py:142
  943.1 10.5 conditional.34
  960.5 47.3 %reduce-scatter.16.cloned.1.call-done = bf16[128,4096]{1,0:T(8,128)(2,1)} async-done(((bf16[512,4096]{1,0:T(8,128)(2,1)}), bf16[128,4096]{1,0:T(8,128)(2,1)}) %reduce-scatter.16.cloned.1.call-update) | async-done | bytes 1048592 | tf_op jit(solution)/shard_map/reduce_scatter | solution.py:204
  1011.0 23.3 %collective-permute-done.8 = bf16[128,4096]{1,0:T(8,128)(2,1)S(1)} collective-permute-done((bf16[128,4096]{1,0:T(8,128)(2,1)S(1)}, bf16[128,4096]{1,0:T(8,128)(2,1)S(1)}, u32[]{:S(2)}, u32[]{:S(2)}) %collective-permute-start.8) | collective-permute-done | bytes 1048608 | tf_op jit(solution)/shard_map/ppermute | solution.py:50
  1037.5 46.4 %all-gather.20.cloned.1.call-done = bf16[512,4096]{1,0:T(8,128)(2,1)} async-done(((bf16[128,4096]{1,0:T(8,128)(2,1)}), bf16[512,4096]{1,0:T(8,128)(2,1)}) %all-gather.20.cloned.1.call-update) | async-done | bytes 4194320 | tf_op jit(solution)/shard_map/all_gather | solution.py:142
  1088.5 70.3 %reduce-scatter.18.cloned.1.call-done = bf16[128,4096]{1,0:T(8,128)(2,1)} async-done(((bf16[512,4096]{1,0:T(8,128)(2,1)}), bf16[128,4096]{1,0:T(8,128)(2,1)}) %reduce-scatter.18.cloned.1.call-update) | async-done | bytes 1048592 | tf_op jit(solution)/shard_map/reduce_scatter | solution.py:204
  1161.9 23.3 %collective-permute-done.10 = bf16[128,4096]{1,0:T(8,128)(2,1)S(1)} collective-permute-done((bf16[128,4096]{1,0:T(8,128)(2,1)S(1)}, bf16[128,4096]{1,0:T(8,128)(2,1)S(1)}, u32[]{:S(2)}, u32[]{:S(2)}) %collective-permute-start.10) | collective-permute-done | bytes 1048608 | tf_op jit(solution)/shard_map/ppermute | solution.py:50
  1188.5 46.4 %all-gather.22.cloned.1.call-done = bf16[512,4096]{1,0:T(8,128)(2,1)} async-done(((bf16[128,4096]{1,0:T(8,128)(2,1)}), bf16[512,4096]{1,0:T(8,128)(2,1)}) %all-gather.22.cloned.1.call-update) | async-done | bytes 4194320 | tf_op jit(solution)/shard_map/all_gather | solution.py:142
  1237.8 65.9 %reduce-scatter.20.cloned.1.call-done = bf16[128,4096]{1,0:T(8,128)(2,1)} async-done(((bf16[512,4096]{1,0:T(8,128)(2,1)}), bf16[128,4096]{1,0:T(8,128)(2,1)}) %reduce-scatter.20.cloned.1.call-update) | async-done | bytes 1048592 | tf_op jit(solution)/shard_map/reduce_scatter | solution.py:204
  1306.9 23.3 %collective-permute-done.12 = bf16[128,4096]{1,0:T(8,128)(2,1)S(1)} collective-permute-done((bf16[128,4096]{1,0:T(8,128)(2,1)S(1)}, bf16[128,4096]{1,0:T(8,128)(2,1)S(1)}, u32[]{:S(2)}, u32[]{:S(2)}) %collective-permute-start.12) | collective-permute-done | bytes 1048608 | tf_op jit(solution)/shard_map/ppermute | solution.py:50
  1332.3 26.3 %psum.28 = s32[]{:T(128)} all-reduce(s32[]{:T(128)} %reduce_sum.242), channel_id=1, replica_groups=mesh['section'=4,'dp_0'=4,'dp_1'=2,'mp'=4] {'section'}, use_global_device_ids=true, to_apply=%region_84.85 | all-reduce | flops 1 | bytes 8 | tf_op jit(solution)/shard_map/psum | solution.py:55
  (310 shorter events, 389.6 us)
Async XLA Ops:
  7.2 75.4 %all-gather.24.cloned.1.call-start = ((), (), s32[]{:S(2)}) async-start(), calls=%async_computation.25 | async-start | bytes 15138816 | tf_op jit(solution)/shard_map/all_gather | solution.py:39
  113.6 54.6 %all-to-all-start = ((bf16[4,512,1024]{2,1,0:T(8,128)(2,1)}), bf16[4,512,1024]{2,1,0:T(8,128)(2,1)}, u32[]{:S(2)}, u32[]{:S(2)}) async-start(bf16[4,512,1024]{2,1,0:T(8,128)(2,1)} %broadcast_in_dim.76), calls=%async_computation | async-start | bytes 8388608 | tf_op jit(solution)/shard_map/all_to_all | solution.py:23
  183.6 54.1 %all-to-all-start.1 = ((bf16[4,512,1024]{2,1,0:T(8,128)(2,1)}), bf16[4,512,1024]{2,1,0:T(8,128)(2,1)}, u32[]{:S(2)}, u32[]{:S(2)}) async-start(bf16[4,512,1024]{2,1,0:T(8,128)(2,1)} %broadcast_in_dim.85), calls=%async_computation.1 | async-start | bytes 8388608 | tf_op jit(solution)/shard_map/all_to_all | solution.py:23
  262.4 17.1 %all-to-all-start.3 = ((bf16[4,128,1024]{2,1,0:T(8,128)(2,1)}), bf16[4,128,1024]{2,1,0:T(8,128)(2,1)}, u32[]{:S(2)}, u32[]{:S(2)}) async-start(bf16[4,128,1024]{2,1,0:T(8,128)(2,1)} %bitcast.135), calls=%async_computation.3 | async-start | bytes 2097152 | tf_op jit(solution)/shard_map/all_to_all | solution.py:289
  266.8 65.7 %all-gather.10.cloned.1.call-start = ((), (), s32[]{:S(2)}) async-start(), calls=%async_computation.11 | async-start | bytes 5242880 | tf_op jit(solution)/shard_map/all_gather | solution.py:142
  285.5 119.2 %reduce-scatter.8.cloned.1.call-start = ((), (), s32[]{:S(2)}) async-start(), calls=%async_computation.12 | async-start | bytes 5242880 | tf_op jit(solution)/shard_map/reduce_scatter | solution.py:204
  336.9 144.5 %all-gather.12.cloned.1.call-start = ((), (), s32[]{:S(2)}) async-start(), calls=%async_computation.13 | async-start | bytes 5242880 | tf_op jit(solution)/shard_map/all_gather | solution.py:142
  406.8 24.9 %collective-permute-start = (bf16[128,4096]{1,0:T(8,128)(2,1)S(1)}, bf16[128,4096]{1,0:T(8,128)(2,1)S(1)}, u32[]{:S(2)}, u32[]{:S(2)}) collective-permute-start(bf16[128,4096]{1,0:T(8,128)(2,1)S(1)} %fusion.241), channel_id=1, source_target_pairs={{0,32},{32,64},{64,96},{96,0},{1,33},{33,65},{65,97},{97,1},{2,34}... | collective-permute-start | bytes 3145736 | tf_op jit(solution)/shard_map/ppermute | solution.py:50
  433.4 121.5 %reduce-scatter.10.cloned.1.call-start = ((), (), s32[]{:S(2)}) async-start(), calls=%async_computation.14 | async-start | bytes 5242880 | tf_op jit(solution)/shard_map/reduce_scatter | solution.py:204
  433.4 58.2 %collective-permute-start.1 = (s32[512]{0:T(512)S(1)}, s32[512]{0:T(512)S(1)}, u32[]{:S(2)}, u32[]{:S(2)}) collective-permute-start(s32[512]{0:T(512)S(1)} %bitcast.536), channel_id=1, source_target_pairs={{0,32},{32,64},{64,96},{96,0},{1,33},{33,65},{65,97},{97,1},{2,34}... | collective-permute-start | bytes 6152 | tf_op jit(solution)/shard_map/ppermute | solution.py:50
  509.2 121.9 %all-gather.14.cloned.1.call-start = ((), (), s32[]{:S(2)}) async-start(), calls=%async_computation.15 | async-start | bytes 5242880 | tf_op jit(solution)/shard_map/all_gather | solution.py:142
  556.4 24.9 %collective-permute-start.2 = (bf16[128,4096]{1,0:T(8,128)(2,1)S(1)}, bf16[128,4096]{1,0:T(8,128)(2,1)S(1)}, u32[]{:S(2)}, u32[]{:S(2)}) collective-permute-start(bf16[128,4096]{1,0:T(8,128)(2,1)S(1)} %fusion.240), channel_id=1, source_target_pairs={{0,32},{32,64},{64,96},{96,0},{1,33},{33,65},{65,97},{97,1},{2,34}... | collective-permute-start | bytes 3145736 | tf_op jit(solution)/shard_map/ppermute | solution.py:50
  583.0 122.9 %reduce-scatter.12.cloned.1.call-start = ((), (), s32[]{:S(2)}) async-start(), calls=%async_computation.16 | async-start | bytes 5242880 | tf_op jit(solution)/shard_map/reduce_scatter | solution.py:204
  583.0 58.2 %collective-permute-start.3 = (s32[512]{0:T(512)S(1)}, s32[512]{0:T(512)S(1)}, u32[]{:S(2)}, u32[]{:S(2)}) collective-permute-start(s32[512]{0:T(512)S(1)} %collective-permute-done.1), channel_id=1, source_target_pairs={{0,32},{32,64},{64,96},{96,0},{1,33},{33,65},{65,97},{97,1},{2,34}... | collective-permute-start | bytes 6152 | tf_op jit(solution)/shard_map/ppermute | solution.py:50
  658.5 123.4 %all-gather.16.cloned.1.call-start = ((), (), s32[]{:S(2)}) async-start(), calls=%async_computation.17 | async-start | bytes 5242880 | tf_op jit(solution)/shard_map/all_gather | solution.py:142
  707.3 24.9 %collective-permute-start.4 = (bf16[128,4096]{1,0:T(8,128)(2,1)S(1)}, bf16[128,4096]{1,0:T(8,128)(2,1)S(1)}, u32[]{:S(2)}, u32[]{:S(2)}) collective-permute-start(bf16[128,4096]{1,0:T(8,128)(2,1)S(1)} %fusion.239), channel_id=1, source_target_pairs={{0,32},{32,64},{64,96},{96,0},{1,33},{33,65},{65,97},{97,1},{2,34}... | collective-permute-start | bytes 3145736 | tf_op jit(solution)/shard_map/ppermute | solution.py:50
  733.9 122.9 %reduce-scatter.14.cloned.1.call-start = ((), (), s32[]{:S(2)}) async-start(), calls=%async_computation.18 | async-start | bytes 5242880 | tf_op jit(solution)/shard_map/reduce_scatter | solution.py:204
  733.9 58.4 %collective-permute-start.5 = (s32[512]{0:T(512)S(1)}, s32[512]{0:T(512)S(1)}, u32[]{:S(2)}, u32[]{:S(2)}) collective-permute-start(s32[512]{0:T(512)S(1)} %collective-permute-done.3), channel_id=1, source_target_pairs={{0,32},{32,64},{64,96},{96,0},{1,33},{33,65},{65,97},{97,1},{2,34}... | collective-permute-start | bytes 6152 | tf_op jit(solution)/shard_map/ppermute | solution.py:50
  809.5 123.4 %all-gather.18.cloned.1.call-start = ((), (), s32[]{:S(2)}) async-start(), calls=%async_computation.19 | async-start | bytes 5242880 | tf_op jit(solution)/shard_map/all_gather | solution.py:142
  858.4 24.9 %collective-permute-start.6 = (bf16[128,4096]{1,0:T(8,128)(2,1)S(1)}, bf16[128,4096]{1,0:T(8,128)(2,1)S(1)}, u32[]{:S(2)}, u32[]{:S(2)}) collective-permute-start(bf16[128,4096]{1,0:T(8,128)(2,1)S(1)} %fusion.238), channel_id=1, source_target_pairs={{0,32},{32,64},{64,96},{96,0},{1,33},{33,65},{65,97},{97,1},{2,34}... | collective-permute-start | bytes 3145736 | tf_op jit(solution)/shard_map/ppermute | solution.py:50
  884.9 122.9 %reduce-scatter.16.cloned.1.call-start = ((), (), s32[]{:S(2)}) async-start(), calls=%async_computation.20 | async-start | bytes 5242880 | tf_op jit(solution)/shard_map/reduce_scatter | solution.py:204
  884.9 58.2 %collective-permute-start.7 = (s32[512]{0:T(512)S(1)}, s32[512]{0:T(512)S(1)}, u32[]{:S(2)}, u32[]{:S(2)}) collective-permute-start(s32[512]{0:T(512)S(1)} %collective-permute-done.5), channel_id=1, source_target_pairs={{0,32},{32,64},{64,96},{96,0},{1,33},{33,65},{65,97},{97,1},{2,34}... | collective-permute-start | bytes 6152 | tf_op jit(solution)/shard_map/ppermute | solution.py:50
  960.5 123.4 %all-gather.20.cloned.1.call-start = ((), (), s32[]{:S(2)}) async-start(), calls=%async_computation.21 | async-start | bytes 5242880 | tf_op jit(solution)/shard_map/all_gather | solution.py:142
  1009.3 24.9 %collective-permute-start.8 = (bf16[128,4096]{1,0:T(8,128)(2,1)S(1)}, bf16[128,4096]{1,0:T(8,128)(2,1)S(1)}, u32[]{:S(2)}, u32[]{:S(2)}) collective-permute-start(bf16[128,4096]{1,0:T(8,128)(2,1)S(1)} %fusion.237), channel_id=1, source_target_pairs={{0,32},{32,64},{64,96},{96,0},{1,33},{33,65},{65,97},{97,1},{2,34}... | collective-permute-start | bytes 3145736 | tf_op jit(solution)/shard_map/ppermute | solution.py:50
  1035.9 122.9 %reduce-scatter.18.cloned.1.call-start = ((), (), s32[]{:S(2)}) async-start(), calls=%async_computation.22 | async-start | bytes 5242880 | tf_op jit(solution)/shard_map/reduce_scatter | solution.py:204
  1035.9 48.9 %collective-permute-start.9 = (s32[512]{0:T(512)S(1)}, s32[512]{0:T(512)S(1)}, u32[]{:S(2)}, u32[]{:S(2)}) collective-permute-start(s32[512]{0:T(512)S(1)} %collective-permute-done.7), channel_id=1, source_target_pairs={{0,32},{32,64},{64,96},{96,0},{1,33},{33,65},{65,97},{97,1},{2,34}... | collective-permute-start | bytes 6152 | tf_op jit(solution)/shard_map/ppermute | solution.py:50
  1088.4 146.5 %all-gather.22.cloned.1.call-start = ((), (), s32[]{:S(2)}) async-start(), calls=%async_computation.23 | async-start | bytes 5242880 | tf_op jit(solution)/shard_map/all_gather | solution.py:142
  1160.3 24.9 %collective-permute-start.10 = (bf16[128,4096]{1,0:T(8,128)(2,1)S(1)}, bf16[128,4096]{1,0:T(8,128)(2,1)S(1)}, u32[]{:S(2)}, u32[]{:S(2)}) collective-permute-start(bf16[128,4096]{1,0:T(8,128)(2,1)S(1)} %fusion.236), channel_id=1, source_target_pairs={{0,32},{32,64},{64,96},{96,0},{1,33},{33,65},{65,97},{97,1},{2,34}... | collective-permute-start | bytes 3145736 | tf_op jit(solution)/shard_map/ppermute | solution.py:50
  1186.8 116.9 %reduce-scatter.20.cloned.1.call-start = ((), (), s32[]{:S(2)}) async-start(), calls=%async_computation.24 | async-start | bytes 5242880 | tf_op jit(solution)/shard_map/reduce_scatter | solution.py:204
  1186.9 48.3 %collective-permute-start.11 = (s32[512]{0:T(512)S(1)}, s32[512]{0:T(512)S(1)}, u32[]{:S(2)}, u32[]{:S(2)}) collective-permute-start(s32[512]{0:T(512)S(1)} %collective-permute-done.9), channel_id=1, source_target_pairs={{0,32},{32,64},{64,96},{96,0},{1,33},{33,65},{65,97},{97,1},{2,34}... | collective-permute-start | bytes 6152 | tf_op jit(solution)/shard_map/ppermute | solution.py:50
  1305.3 24.9 %collective-permute-start.12 = (bf16[128,4096]{1,0:T(8,128)(2,1)S(1)}, bf16[128,4096]{1,0:T(8,128)(2,1)S(1)}, u32[]{:S(2)}, u32[]{:S(2)}) collective-permute-start(bf16[128,4096]{1,0:T(8,128)(2,1)S(1)} %fusion.235), channel_id=1, source_target_pairs={{0,32},{32,64},{64,96},{96,0},{1,33},{33,65},{65,97},{97,1},{2,34}... | collective-permute-start | bytes 3145736 | tf_op jit(solution)/shard_map/ppermute | solution.py:50
  1330.1 49.6 %collective-permute-start.13 = (bf16[128,4096]{1,0:T(8,128)(2,1)S(1)}, bf16[128,4096]{1,0:T(8,128)(2,1)S(1)}, u32[]{:S(2)}, u32[]{:S(2)}) collective-permute-start(bf16[128,4096]{1,0:T(8,128)(2,1)S(1)} %collective-permute-done.12), channel_id=1, source_target_pairs={{0,32},{32,64},{64,96},{96,0},{1,33},{33,65},{65,97},{97,1},{2,34}... | collective-permute-start | bytes 3145736 | tf_op jit(solution)/shard_map/ppermute | solution.py:50
  (26 other events, 291.0 us)
Sparse Core Ops, SparseCore 0:
  13.2 69.3 all-gather.23
  285.6 46.8 all-gather.9
  337.1 67.6 reduce-scatter.7
  433.5 47.9 all-gather.11
  509.3 45.5 reduce-scatter.9
  583.1 47.8 all-gather.13
  658.6 47.1 reduce-scatter.11
  734.0 47.8 all-gather.15
  809.6 47.1 reduce-scatter.13
  885.0 47.9 all-gather.17
  960.6 47.1 reduce-scatter.15
  1036.0 47.8 all-gather.19
  1088.5 70.1 reduce-scatter.17
  1187.0 47.8 all-gather.21
  1237.9 65.7 reduce-scatter.19
where the time goes:
time: 1400 us; the launch traced here: 1390 us
  waiting for transfers between devices  1020 us (73%)
  local copies, waits for them, and re-layouts  106 us (8%)
  matrix products  101 us (7%)
  other arithmetic  51.4 us (4%)
  starting transfers between devices  48.4 us (3%)
  blocking collectives  46.2 us (3%)
  between operations  15.6 us (1%)
    reduce_scatter x7, waiting for transfers between devices, decoder_layer(): lax.psum_scatter(lax.cond(active, out_computed, out_skipped, mixed).astyp...  386 us
    all_gather x7, waiting for transfers between devices, decoder_layer(): piece = lax.all_gather(normed, 'mp', axis=0, tiled=True)  325 us
    ppermute x14, waiting for transfers between devices, shifted(): return lax.ppermute(value, axis, pairs)  163 us
    all_gather x1, waiting for transfers between devices, one_gather(): lines, at, done = (lax.all_gather(flat, axis), 0, [])  66.2 us
    all_to_all x2, waiting for transfers between devices, copy_for_each(): return lax.all_to_all(copies, axis, split_axis=0, concat_axis=0, tiled=True)  59.1 us
    psum x4, blocking collectives, over_axes(): array = lax.psum(array, axis)  46.2 us
  transfers between devices with their start and end apart: 33, of which 26 were waited for; matrix products, arithmetic and copies ran while one was open for 6% of the time, Pallas kernels for 0%

commit v1 on v0

--- a/solution.py
+++ b/solution.py
@@ -16,6 +16,12 @@
 EPS = 1e-05
 ROPE_BASE = 500000.0
 BLOCKED = -1e30
+
+
+def direct_members_all_on_mesh(xs, row_dim):
+    xs = jnp.moveaxis(xs, 0, row_dim)
+    back = xs.shape
+    return xs.reshape(*back[:row_dim], back[row_dim] * back[row_dim + 1], *back[row_dim + 2 :])
 
 
 def copy_for_each(array, axis):
@@ -139,7 +145,27 @@
     pair_width = w_kv.shape[2]
     joined_width = query_width + 2 * pair_width
     model_width = w_out.shape[1]
-    piece = lax.all_gather(normed, "mp", axis=0, tiled=True)
+    ledger = []
+    shares = lax.psum(1, "mp")
+    for no in [*range(shares)]:
+        ledger.append((no, (no + 1) % shares))
+    arrivals = []
+    for m, to_i in ledger:
+        arrivals.append((to_i, m))
+    out_arr, now = ([], [])
+    for dev_i in tuple(range(shares - 1)):
+        if dev_i % 2 == 0:
+            block_next = lax.ppermute(out_arr[-1] if out_arr else normed, "mp", ledger)
+            out_arr.append(block_next)
+        else:
+            arr_out = lax.ppermute(now[-1] if now else normed, "mp", arrivals)
+            now.append(arr_out)
+    local_part = jnp.stack([*out_arr[::-1], normed, *now])
+    low = lax.axis_index("mp")
+    met_up = len(out_arr)
+    w1 = low - met_up
+    local_part = local_part[(jnp.arange(shares) - w1) % shares]
+    piece = direct_members_all_on_mesh(local_part, 0)
     row_count = piece.shape[0]
 
     def project_computed(rows):

time: 1400 us -> 1460 us (1.043)
  other arithmetic: 51.4 us -> 78.1 us
  local copies, waits for them, and re-layouts: 106 us -> 128 us
  starting transfers between devices: 48.4 us -> 65.3 us
    all_gather x7 -> x0, waiting for transfers between devices: 325 us -> none  [decoder_layer(): piece = lax.all_gather(normed, 'mp', axis=0, tiled=True)]
    ppermute x0 -> x21, waiting for transfers between devices: none -> 303 us  [the longest x14 301 us: decoder_layer(): block_next = lax.ppermute(out_arr[-1] if out_arr else normed, 'mp', ledger)]
    another operation x8 -> x21, other arithmetic: 2.98 us -> 30.7 us  [the longest x13 27.8 us: decoder_layer(): local_part = jnp.stack([*out_arr[::-1], normed, *now])]
    ppermute x0 -> x21, starting transfers between devices: none -> 22.9 us  [the longest x7 20.6 us: decoder_layer(): arr_out = lax.ppermute(now[-1] if now else normed, 'mp', arrivals)]
    gather x0 -> x4, local copies, waits for them, and re-layouts: none -> 20 us  [decoder_layer(): local_part = local_part[(jnp.arange(shares) - w1) % shares]]
  transfers between devices with their start and end apart: 33 -> 47, of which waited for: 26 -> 34; matrix products, arithmetic and copies ran while one was open for 6% -> 10% of each run, Pallas kernels for 0% -> 0%
where the time goes in v1:
time: 1460 us; the launch traced here: 1450 us
  waiting for transfers between devices  1010 us (69%)
  local copies, waits for them, and re-layouts  128 us (9%)
  matrix products  105 us (7%)
  other arithmetic  78.1 us (5%)
  starting transfers between devices  65.3 us (4%)
  blocking collectives  46.2 us (3%)
  between operations  15.7 us (1%)
    reduce_scatter x7, waiting for transfers between devices, decoder_layer(): lax.psum_scatter(lax.cond(active, out_computed, out_skipped, mixed).astyp...  398 us
    ppermute x14, waiting for transfers between devices, decoder_layer(): block_next = lax.ppermute(out_arr[-1] if out_arr else normed, 'mp', ledger)  301 us
    ppermute x14, waiting for transfers between devices, shifted(): return lax.ppermute(value, axis, pairs)  163 us
    all_gather x1, waiting for transfers between devices, one_gather(): lines, at, done = (lax.all_gather(flat, axis), 0, [])  66.2 us
    all_to_all x2, waiting for transfers between devices, copy_for_each(): return lax.all_to_all(copies, axis, split_axis=0, concat_axis=0, tiled=True)  59.1 us
    psum x4, blocking collectives, over_axes(): array = lax.psum(array, axis)  46.2 us
  transfers between devices with their start and end apart: 47, of which 34 were waited for; matrix products, arithmetic and copies ran while one was open for 10% of the time, Pallas kernels for 0%

profile of v1, /device:TPU:32, one launch (start us, length us, event | category | flops | bytes accessed | tf_op | source)
XLA Modules:
  0.0 1448.3 jit_solution(13929155473218523133)
XLA Ops:
  16.4 66.2 %all-gather.3.cloned.1.call-done = bf16[7340032]{0:T(1024)(128)(2,1)} async-done(((bf16[229376]{0:T(1024)(128)(2,1)}), bf16[7340032]{0:T(1024)(128)(2,1)}) %all-gather.3.cloned.1.call-update) | async-done | bytes 14680080 | tf_op jit(solution)/shard_map/all_gather | solution.py:45
  141.2 27.2 %all-to-all-done = bf16[4,512,1024]{2,1,0:T(8,128)(2,1)} async-done(((bf16[4,512,1024]{2,1,0:T(8,128)(2,1)}), bf16[4,512,1024]{2,1,0:T(8,128)(2,1)}, u32[]{:S(2)}, u32[]{:S(2)}) %all-to-all-start) | async-done | bytes 4194336 | tf_op jit(solution)/shard_map/all_to_all | solution.py:29
  205.7 31.9 %all-to-all-done.1 = bf16[4,512,1024]{2,1,0:T(8,128)(2,1)} async-done(((bf16[4,512,1024]{2,1,0:T(8,128)(2,1)}), bf16[4,512,1024]{2,1,0:T(8,128)(2,1)}, u32[]{:S(2)}, u32[]{:S(2)}) %all-to-all-start.1) | async-done | bytes 4194336 | tf_op jit(solution)/shard_map/all_to_all | solution.py:29
  309.1 16.8 %collective-permute-done.1 = bf16[128,4096]{1,0:T(8,128)(2,1)} collective-permute-done((bf16[128,4096]{1,0:T(8,128)(2,1)}, bf16[128,4096]{1,0:T(8,128)(2,1)}, u32[]{:S(2)}, u32[]{:S(2)}) %collective-permute-start.1) | collective-permute-done | bytes 1048608 | tf_op jit(solution)/shard_map/ppermute | solution.py:158
  334.5 72.8 %reduce-scatter.8.cloned.1.call-done = bf16[128,4096]{1,0:T(8,128)(2,1)} async-done(((bf16[512,4096]{1,0:T(8,128)(2,1)}), bf16[128,4096]{1,0:T(8,128)(2,1)}) %reduce-scatter.8.cloned.1.call-update) | async-done | bytes 1048592 | tf_op jit(solution)/shard_map/reduce_scatter | solution.py:230
  411.1 23.3 %collective-permute-done.3 = bf16[128,4096]{1,0:T(8,128)(2,1)S(1)} collective-permute-done((bf16[128,4096]{1,0:T(8,128)(2,1)S(1)}, bf16[128,4096]{1,0:T(8,128)(2,1)S(1)}, u32[]{:S(2)}, u32[]{:S(2)}) %collective-permute-start.3) | collective-permute-done | bytes 1048608 | tf_op jit(solution)/shard_map/ppermute | solution.py:56
  439.2 22.3 %collective-permute-done.5 = bf16[128,4096]{1,0:T(8,128)(2,1)} collective-permute-done((bf16[128,4096]{1,0:T(8,128)(2,1)}, bf16[128,4096]{1,0:T(8,128)(2,1)}, u32[]{:S(2)}, u32[]{:S(2)}) %collective-permute-start.5) | collective-permute-done | bytes 1048608 | tf_op jit(solution)/shard_map/ppermute | solution.py:158
  463.3 22.8 %collective-permute-done.6 = bf16[128,4096]{1,0:T(8,128)(2,1)} collective-permute-done((bf16[128,4096]{1,0:T(8,128)(2,1)}, bf16[128,4096]{1,0:T(8,128)(2,1)}, u32[]{:S(2)}, u32[]{:S(2)}) %collective-permute-start.6) | collective-permute-done | bytes 1048608 | tf_op jit(solution)/shard_map/ppermute | solution.py:158
  522.7 44.3 %reduce-scatter.10.cloned.1.call-done = bf16[128,4096]{1,0:T(8,128)(2,1)} async-done(((bf16[512,4096]{1,0:T(8,128)(2,1)}), bf16[128,4096]{1,0:T(8,128)(2,1)}) %reduce-scatter.10.cloned.1.call-update) | async-done | bytes 1048592 | tf_op jit(solution)/shard_map/reduce_scatter | solution.py:230
  570.2 23.3 %collective-permute-done.8 = bf16[128,4096]{1,0:T(8,128)(2,1)S(1)} collective-permute-done((bf16[128,4096]{1,0:T(8,128)(2,1)S(1)}, bf16[128,4096]{1,0:T(8,128)(2,1)S(1)}, u32[]{:S(2)}, u32[]{:S(2)}) %collective-permute-start.8) | collective-permute-done | bytes 1048608 | tf_op jit(solution)/shard_map/ppermute | solution.py:56
  598.3 22.3 %collective-permute-done.10 = bf16[128,4096]{1,0:T(8,128)(2,1)} collective-permute-done((bf16[128,4096]{1,0:T(8,128)(2,1)}, bf16[128,4096]{1,0:T(8,128)(2,1)}, u32[]{:S(2)}, u32[]{:S(2)}) %collective-permute-start.10) | collective-permute-done | bytes 1048608 | tf_op jit(solution)/shard_map/ppermute | solution.py:158
  622.5 22.8 %collective-permute-done.11 = bf16[128,4096]{1,0:T(8,128)(2,1)} collective-permute-done((bf16[128,4096]{1,0:T(8,128)(2,1)}, bf16[128,4096]{1,0:T(8,128)(2,1)}, u32[]{:S(2)}, u32[]{:S(2)}) %collective-permute-start.11) | collective-permute-done | bytes 1048608 | tf_op jit(solution)/shard_map/ppermute | solution.py:158
  682.3 45.3 %reduce-scatter.12.cloned.1.call-done = bf16[128,4096]{1,0:T(8,128)(2,1)} async-done(((bf16[512,4096]{1,0:T(8,128)(2,1)}), bf16[128,4096]{1,0:T(8,128)(2,1)}) %reduce-scatter.12.cloned.1.call-update) | async-done | bytes 1048592 | tf_op jit(solution)/shard_map/reduce_scatter | solution.py:230
  730.7 23.3 %collective-permute-done.13 = bf16[128,4096]{1,0:T(8,128)(2,1)S(1)} collective-permute-done((bf16[128,4096]{1,0:T(8,128)(2,1)S(1)}, bf16[128,4096]{1,0:T(8,128)(2,1)S(1)}, u32[]{:S(2)}, u32[]{:S(2)}) %collective-permute-start.13) | collective-permute-done | bytes 1048608 | tf_op jit(solution)/shard_map/ppermute | solution.py:56
  758.8 22.3 %collective-permute-done.15 = bf16[128,4096]{1,0:T(8,128)(2,1)} collective-permute-done((bf16[128,4096]{1,0:T(8,128)(2,1)}, bf16[128,4096]{1,0:T(8,128)(2,1)}, u32[]{:S(2)}, u32[]{:S(2)}) %collective-permute-start.15) | collective-permute-done | bytes 1048608 | tf_op jit(solution)/shard_map/ppermute | solution.py:158
  783.0 22.8 %collective-permute-done.16 = bf16[128,4096]{1,0:T(8,128)(2,1)} collective-permute-done((bf16[128,4096]{1,0:T(8,128)(2,1)}, bf16[128,4096]{1,0:T(8,128)(2,1)}, u32[]{:S(2)}, u32[]{:S(2)}) %collective-permute-start.16) | collective-permute-done | bytes 1048608 | tf_op jit(solution)/shard_map/ppermute | solution.py:158
  842.3 45.7 %reduce-scatter.14.cloned.1.call-done = bf16[128,4096]{1,0:T(8,128)(2,1)} async-done(((bf16[512,4096]{1,0:T(8,128)(2,1)}), bf16[128,4096]{1,0:T(8,128)(2,1)}) %reduce-scatter.14.cloned.1.call-update) | async-done | bytes 1048592 | tf_op jit(solution)/shard_map/reduce_scatter | solution.py:230
  891.2 23.3 %collective-permute-done.18 = bf16[128,4096]{1,0:T(8,128)(2,1)S(1)} collective-permute-done((bf16[128,4096]{1,0:T(8,128)(2,1)S(1)}, bf16[128,4096]{1,0:T(8,128)(2,1)S(1)}, u32[]{:S(2)}, u32[]{:S(2)}) %collective-permute-start.18) | collective-permute-done | bytes 1048608 | tf_op jit(solution)/shard_map/ppermute | solution.py:56
  919.3 22.3 %collective-permute-done.20 = bf16[128,4096]{1,0:T(8,128)(2,1)} collective-permute-done((bf16[128,4096]{1,0:T(8,128)(2,1)}, bf16[128,4096]{1,0:T(8,128)(2,1)}, u32[]{:S(2)}, u32[]{:S(2)}) %collective-permute-start.20) | collective-permute-done | bytes 1048608 | tf_op jit(solution)/shard_map/ppermute | solution.py:158
  943.5 22.8 %collective-permute-done.21 = bf16[128,4096]{1,0:T(8,128)(2,1)} collective-permute-done((bf16[128,4096]{1,0:T(8,128)(2,1)}, bf16[128,4096]{1,0:T(8,128)(2,1)}, u32[]{:S(2)}, u32[]{:S(2)}) %collective-permute-start.21) | collective-permute-done | bytes 1048608 | tf_op jit(solution)/shard_map/ppermute | solution.py:158
  969.9 16.5 %conditional.33 = (bf16[512,768]{0,1:T(8,128)(2,1)}) conditional(s32[]{:T(128)} %convert_element_type.549, () %tuple.160, (bf16[4,128,4096]{2,1,0:T(8,128)(2,1)}, s32[4,1]{0,1:T(1,128)S(1)}, bf16[4096,512]{0,1:T(8,128)(2,1)}, bf16[2,4096,128]{2,1,0:T(8,128)(2,1)S(1)}) %tuple.347), branch_computations={%region_54.55_spmd, %region_55.56_spmd} | conditional | flops 3226338816 | bytes 50867012 | solution.py:192
  1003.2 45.3 %reduce-scatter.16.cloned.1.call-done = bf16[128,4096]{1,0:T(8,128)(2,1)} async-done(((bf16[512,4096]{1,0:T(8,128)(2,1)}), bf16[128,4096]{1,0:T(8,128)(2,1)}) %reduce-scatter.16.cloned.1.call-update) | async-done | bytes 1048592 | tf_op jit(solution)/shard_map/reduce_scatter | solution.py:230
  1051.7 23.3 %collective-permute-done.23 = bf16[128,4096]{1,0:T(8,128)(2,1)S(1)} collective-permute-done((bf16[128,4096]{1,0:T(8,128)(2,1)S(1)}, bf16[128,4096]{1,0:T(8,128)(2,1)S(1)}, u32[]{:S(2)}, u32[]{:S(2)}) %collective-permute-start.23) | collective-permute-done | bytes 1048608 | tf_op jit(solution)/shard_map/ppermute | solution.py:56
  1079.8 22.3 %collective-permute-done.25 = bf16[128,4096]{1,0:T(8,128)(2,1)} collective-permute-done((bf16[128,4096]{1,0:T(8,128)(2,1)}, bf16[128,4096]{1,0:T(8,128)(2,1)}, u32[]{:S(2)}, u32[]{:S(2)}) %collective-permute-start.25) | collective-permute-done | bytes 1048608 | tf_op jit(solution)/shard_map/ppermute | solution.py:158
  1104.0 22.8 %collective-permute-done.26 = bf16[128,4096]{1,0:T(8,128)(2,1)} collective-permute-done((bf16[128,4096]{1,0:T(8,128)(2,1)}, bf16[128,4096]{1,0:T(8,128)(2,1)}, u32[]{:S(2)}, u32[]{:S(2)}) %collective-permute-start.26) | collective-permute-done | bytes 1048608 | tf_op jit(solution)/shard_map/ppermute | solution.py:158
  1135.0 74.0 %reduce-scatter.18.cloned.1.call-done = bf16[128,4096]{1,0:T(8,128)(2,1)} async-done(((bf16[512,4096]{1,0:T(8,128)(2,1)}), bf16[128,4096]{1,0:T(8,128)(2,1)}) %reduce-scatter.18.cloned.1.call-update) | async-done | bytes 1048592 | tf_op jit(solution)/shard_map/reduce_scatter | solution.py:230
  1212.1 23.3 %collective-permute-done.28 = bf16[128,4096]{1,0:T(8,128)(2,1)S(1)} collective-permute-done((bf16[128,4096]{1,0:T(8,128)(2,1)S(1)}, bf16[128,4096]{1,0:T(8,128)(2,1)S(1)}, u32[]{:S(2)}, u32[]{:S(2)}) %collective-permute-start.28) | collective-permute-done | bytes 1048608 | tf_op jit(solution)/shard_map/ppermute | solution.py:56
  1240.3 22.3 %collective-permute-done.30 = bf16[128,4096]{1,0:T(8,128)(2,1)} collective-permute-done((bf16[128,4096]{1,0:T(8,128)(2,1)}, bf16[128,4096]{1,0:T(8,128)(2,1)}, u32[]{:S(2)}, u32[]{:S(2)}) %collective-permute-start.30) | collective-permute-done | bytes 1048608 | tf_op jit(solution)/shard_map/ppermute | solution.py:158
  1264.5 22.7 %collective-permute-done.31 = bf16[128,4096]{1,0:T(8,128)(2,1)} collective-permute-done((bf16[128,4096]{1,0:T(8,128)(2,1)}, bf16[128,4096]{1,0:T(8,128)(2,1)}, u32[]{:S(2)}, u32[]{:S(2)}) %collective-permute-start.31) | collective-permute-done | bytes 1048608 | tf_op jit(solution)/shard_map/ppermute | solution.py:158
  1293.8 70.5 %reduce-scatter.20.cloned.1.call-done = bf16[128,4096]{1,0:T(8,128)(2,1)} async-done(((bf16[512,4096]{1,0:T(8,128)(2,1)}), bf16[128,4096]{1,0:T(8,128)(2,1)}) %reduce-scatter.20.cloned.1.call-update) | async-done | bytes 1048592 | tf_op jit(solution)/shard_map/reduce_scatter | solution.py:230
  1367.4 23.3 %collective-permute-done.33 = bf16[128,4096]{1,0:T(8,128)(2,1)S(1)} collective-permute-done((bf16[128,4096]{1,0:T(8,128)(2,1)S(1)}, bf16[128,4096]{1,0:T(8,128)(2,1)S(1)}, u32[]{:S(2)}, u32[]{:S(2)}) %collective-permute-start.33) | collective-permute-done | bytes 1048608 | tf_op jit(solution)/shard_map/ppermute | solution.py:56
  1392.9 26.3 %psum.28 = s32[]{:T(128)} all-reduce(s32[]{:T(128)} %reduce_sum.242), channel_id=1, replica_groups=mesh['section'=4,'dp_0'=4,'dp_1'=2,'mp'=4] {'section'}, use_global_device_ids=true, to_apply=%region_84.85 | all-reduce | flops 1 | bytes 8 | tf_op jit(solution)/shard_map/psum | solution.py:61
  (349 shorter events, 557.7 us)
Async XLA Ops:
  7.2 75.4 %all-gather.3.cloned.1.call-start = ((), (), s32[]{:S(2)}) async-start(), calls=%async_computation.18 | async-start | bytes 15138816 | tf_op jit(solution)/shard_map/all_gather | solution.py:45
  113.6 54.8 %all-to-all-start = ((bf16[4,512,1024]{2,1,0:T(8,128)(2,1)}), bf16[4,512,1024]{2,1,0:T(8,128)(2,1)}, u32[]{:S(2)}, u32[]{:S(2)}) async-start(bf16[4,512,1024]{2,1,0:T(8,128)(2,1)} %broadcast_in_dim.78), calls=%async_computation | async-start | bytes 8388608 | tf_op jit(solution)/shard_map/all_to_all | solution.py:29
  183.8 53.8 %all-to-all-start.1 = ((bf16[4,512,1024]{2,1,0:T(8,128)(2,1)}), bf16[4,512,1024]{2,1,0:T(8,128)(2,1)}, u32[]{:S(2)}, u32[]{:S(2)}) async-start(bf16[4,512,1024]{2,1,0:T(8,128)(2,1)} %broadcast_in_dim.87), calls=%async_computation.1 | async-start | bytes 8388608 | tf_op jit(solution)/shard_map/all_to_all | solution.py:29
  266.1 141.2 %reduce-scatter.8.cloned.1.call-start = ((), (), s32[]{:S(2)}) async-start(), calls=%async_computation.11 | async-start | bytes 5242880 | tf_op jit(solution)/shard_map/reduce_scatter | solution.py:230
  334.5 232.5 %reduce-scatter.10.cloned.1.call-start = ((), (), s32[]{:S(2)}) async-start(), calls=%async_computation.12 | async-start | bytes 5242880 | tf_op jit(solution)/shard_map/reduce_scatter | solution.py:230
  409.4 24.9 %collective-permute-start.3 = (bf16[128,4096]{1,0:T(8,128)(2,1)S(1)}, bf16[128,4096]{1,0:T(8,128)(2,1)S(1)}, u32[]{:S(2)}, u32[]{:S(2)}) collective-permute-start(bf16[128,4096]{1,0:T(8,128)(2,1)S(1)} %fusion.241), channel_id=1, source_target_pairs={{0,32},{32,64},{64,96},{96,0},{1,33},{33,65},{65,97},{97,1},{2,34}... | collective-permute-start | bytes 3145736 | tf_op jit(solution)/shard_map/ppermute | solution.py:56
  436.0 25.5 %collective-permute-start.5 = (bf16[128,4096]{1,0:T(8,128)(2,1)}, bf16[128,4096]{1,0:T(8,128)(2,1)}, u32[]{:S(2)}, u32[]{:S(2)}) collective-permute-start(bf16[128,4096]{1,0:T(8,128)(2,1)} %fusion.205), channel_id=1, source_target_pairs={{0,1},{1,2},{2,3},{3,0},{4,5},{5,6},{6,7},{7,4},{8,9},{9,10},{10,1... | collective-permute-start | bytes 3145736 | tf_op jit(solution)/shard_map/ppermute | solution.py:158
  436.2 27.1 %collective-permute-start.7 = (bf16[128,4096]{1,0:T(8,128)(2,1)}, bf16[128,4096]{1,0:T(8,128)(2,1)}, u32[]{:S(2)}, u32[]{:S(2)}) collective-permute-start(bf16[128,4096]{1,0:T(8,128)(2,1)} %fusion.205), channel_id=1, source_target_pairs={{1,0},{2,1},{3,2},{0,3},{5,4},{6,5},{7,6},{4,7},{9,8},{10,9},{11,1... | collective-permute-start | bytes 3145736 | tf_op jit(solution)/shard_map/ppermute | solution.py:161
  461.5 44.7 %collective-permute-start.4 = (s32[512]{0:T(512)S(1)}, s32[512]{0:T(512)S(1)}, u32[]{:S(2)}, u32[]{:S(2)}) collective-permute-start(s32[512]{0:T(512)S(1)} %bitcast.653), channel_id=1, source_target_pairs={{0,32},{32,64},{64,96},{96,0},{1,33},{33,65},{65,97},{97,1},{2,34}... | collective-permute-start | bytes 6152 | tf_op jit(solution)/shard_map/ppermute | solution.py:56
  522.6 204.9 %reduce-scatter.12.cloned.1.call-start = ((), (), s32[]{:S(2)}) async-start(), calls=%async_computation.13 | async-start | bytes 5242880 | tf_op jit(solution)/shard_map/reduce_scatter | solution.py:230
  568.6 24.9 %collective-permute-start.8 = (bf16[128,4096]{1,0:T(8,128)(2,1)S(1)}, bf16[128,4096]{1,0:T(8,128)(2,1)S(1)}, u32[]{:S(2)}, u32[]{:S(2)}) collective-permute-start(bf16[128,4096]{1,0:T(8,128)(2,1)S(1)} %fusion.240), channel_id=1, source_target_pairs={{0,32},{32,64},{64,96},{96,0},{1,33},{33,65},{65,97},{97,1},{2,34}... | collective-permute-start | bytes 3145736 | tf_op jit(solution)/shard_map/ppermute | solution.py:56
  595.1 25.5 %collective-permute-start.10 = (bf16[128,4096]{1,0:T(8,128)(2,1)}, bf16[128,4096]{1,0:T(8,128)(2,1)}, u32[]{:S(2)}, u32[]{:S(2)}) collective-permute-start(bf16[128,4096]{1,0:T(8,128)(2,1)} %fusion.209), channel_id=1, source_target_pairs={{0,1},{1,2},{2,3},{3,0},{4,5},{5,6},{6,7},{7,4},{8,9},{9,10},{10,1... | collective-permute-start | bytes 3145736 | tf_op jit(solution)/shard_map/ppermute | solution.py:158
  595.3 27.2 %collective-permute-start.12 = (bf16[128,4096]{1,0:T(8,128)(2,1)}, bf16[128,4096]{1,0:T(8,128)(2,1)}, u32[]{:S(2)}, u32[]{:S(2)}) collective-permute-start(bf16[128,4096]{1,0:T(8,128)(2,1)} %fusion.209), channel_id=1, source_target_pairs={{1,0},{2,1},{3,2},{0,3},{5,4},{6,5},{7,6},{4,7},{9,8},{10,9},{11,1... | collective-permute-start | bytes 3145736 | tf_op jit(solution)/shard_map/ppermute | solution.py:161
  620.6 44.9 %collective-permute-start.9 = (s32[512]{0:T(512)S(1)}, s32[512]{0:T(512)S(1)}, u32[]{:S(2)}, u32[]{:S(2)}) collective-permute-start(s32[512]{0:T(512)S(1)} %collective-permute-done.4), channel_id=1, source_target_pairs={{0,32},{32,64},{64,96},{96,0},{1,33},{33,65},{65,97},{97,1},{2,34}... | collective-permute-start | bytes 6152 | tf_op jit(solution)/shard_map/ppermute | solution.py:56
  681.8 206.2 %reduce-scatter.14.cloned.1.call-start = ((), (), s32[]{:S(2)}) async-start(), calls=%async_computation.14 | async-start | bytes 5242880 | tf_op jit(solution)/shard_map/reduce_scatter | solution.py:230
  755.6 25.5 %collective-permute-start.15 = (bf16[128,4096]{1,0:T(8,128)(2,1)}, bf16[128,4096]{1,0:T(8,128)(2,1)}, u32[]{:S(2)}, u32[]{:S(2)}) collective-permute-start(bf16[128,4096]{1,0:T(8,128)(2,1)} %fusion.213), channel_id=1, source_target_pairs={{0,1},{1,2},{2,3},{3,0},{4,5},{5,6},{6,7},{7,4},{8,9},{9,10},{10,1... | collective-permute-start | bytes 3145736 | tf_op jit(solution)/shard_map/ppermute | solution.py:158
  755.9 27.1 %collective-permute-start.17 = (bf16[128,4096]{1,0:T(8,128)(2,1)}, bf16[128,4096]{1,0:T(8,128)(2,1)}, u32[]{:S(2)}, u32[]{:S(2)}) collective-permute-start(bf16[128,4096]{1,0:T(8,128)(2,1)} %fusion.213), channel_id=1, source_target_pairs={{1,0},{2,1},{3,2},{0,3},{5,4},{6,5},{7,6},{4,7},{9,8},{10,9},{11,1... | collective-permute-start | bytes 3145736 | tf_op jit(solution)/shard_map/ppermute | solution.py:161
  781.1 44.6 %collective-permute-start.14 = (s32[512]{0:T(512)S(1)}, s32[512]{0:T(512)S(1)}, u32[]{:S(2)}, u32[]{:S(2)}) collective-permute-start(s32[512]{0:T(512)S(1)} %collective-permute-done.9), channel_id=1, source_target_pairs={{0,32},{32,64},{64,96},{96,0},{1,33},{33,65},{65,97},{97,1},{2,34}... | collective-permute-start | bytes 6152 | tf_op jit(solution)/shard_map/ppermute | solution.py:56
  842.2 206.3 %reduce-scatter.16.cloned.1.call-start = ((), (), s32[]{:S(2)}) async-start(), calls=%async_computation.15 | async-start | bytes 5242880 | tf_op jit(solution)/shard_map/reduce_scatter | solution.py:230
  889.5 24.9 %collective-permute-start.18 = (bf16[128,4096]{1,0:T(8,128)(2,1)S(1)}, bf16[128,4096]{1,0:T(8,128)(2,1)S(1)}, u32[]{:S(2)}, u32[]{:S(2)}) collective-permute-start(bf16[128,4096]{1,0:T(8,128)(2,1)S(1)} %fusion.238), channel_id=1, source_target_pairs={{0,32},{32,64},{64,96},{96,0},{1,33},{33,65},{65,97},{97,1},{2,34}... | collective-permute-start | bytes 3145736 | tf_op jit(solution)/shard_map/ppermute | solution.py:56
  916.1 25.5 %collective-permute-start.20 = (bf16[128,4096]{1,0:T(8,128)(2,1)}, bf16[128,4096]{1,0:T(8,128)(2,1)}, u32[]{:S(2)}, u32[]{:S(2)}) collective-permute-start(bf16[128,4096]{1,0:T(8,128)(2,1)} %fusion.217), channel_id=1, source_target_pairs={{0,1},{1,2},{2,3},{3,0},{4,5},{5,6},{6,7},{7,4},{8,9},{9,10},{10,1... | collective-permute-start | bytes 3145736 | tf_op jit(solution)/shard_map/ppermute | solution.py:158
  916.3 27.1 %collective-permute-start.22 = (bf16[128,4096]{1,0:T(8,128)(2,1)}, bf16[128,4096]{1,0:T(8,128)(2,1)}, u32[]{:S(2)}, u32[]{:S(2)}) collective-permute-start(bf16[128,4096]{1,0:T(8,128)(2,1)} %fusion.217), channel_id=1, source_target_pairs={{1,0},{2,1},{3,2},{0,3},{5,4},{6,5},{7,6},{4,7},{9,8},{10,9},{11,1... | collective-permute-start | bytes 3145736 | tf_op jit(solution)/shard_map/ppermute | solution.py:161
  941.6 44.9 %collective-permute-start.19 = (s32[512]{0:T(512)S(1)}, s32[512]{0:T(512)S(1)}, u32[]{:S(2)}, u32[]{:S(2)}) collective-permute-start(s32[512]{0:T(512)S(1)} %collective-permute-done.14), channel_id=1, source_target_pairs={{0,32},{32,64},{64,96},{96,0},{1,33},{33,65},{65,97},{97,1},{2,34}... | collective-permute-start | bytes 6152 | tf_op jit(solution)/shard_map/ppermute | solution.py:56
  1002.8 206.2 %reduce-scatter.18.cloned.1.call-start = ((), (), s32[]{:S(2)}) async-start(), calls=%async_computation.16 | async-start | bytes 5242880 | tf_op jit(solution)/shard_map/reduce_scatter | solution.py:230
  1076.6 25.5 %collective-permute-start.25 = (bf16[128,4096]{1,0:T(8,128)(2,1)}, bf16[128,4096]{1,0:T(8,128)(2,1)}, u32[]{:S(2)}, u32[]{:S(2)}) collective-permute-start(bf16[128,4096]{1,0:T(8,128)(2,1)} %fusion.221), channel_id=1, source_target_pairs={{0,1},{1,2},{2,3},{3,0},{4,5},{5,6},{6,7},{7,4},{8,9},{9,10},{10,1... | collective-permute-start | bytes 3145736 | tf_op jit(solution)/shard_map/ppermute | solution.py:158
  1076.8 27.2 %collective-permute-start.27 = (bf16[128,4096]{1,0:T(8,128)(2,1)}, bf16[128,4096]{1,0:T(8,128)(2,1)}, u32[]{:S(2)}, u32[]{:S(2)}) collective-permute-start(bf16[128,4096]{1,0:T(8,128)(2,1)} %fusion.221), channel_id=1, source_target_pairs={{1,0},{2,1},{3,2},{0,3},{5,4},{6,5},{7,6},{4,7},{9,8},{10,9},{11,1... | collective-permute-start | bytes 3145736 | tf_op jit(solution)/shard_map/ppermute | solution.py:161
  1102.1 29.3 %collective-permute-start.24 = (s32[512]{0:T(512)S(1)}, s32[512]{0:T(512)S(1)}, u32[]{:S(2)}, u32[]{:S(2)}) collective-permute-start(s32[512]{0:T(512)S(1)} %collective-permute-done.19), channel_id=1, source_target_pairs={{0,32},{32,64},{64,96},{96,0},{1,33},{33,65},{65,97},{97,1},{2,34}... | collective-permute-start | bytes 6152 | tf_op jit(solution)/shard_map/ppermute | solution.py:56
  1135.0 229.3 %reduce-scatter.20.cloned.1.call-start = ((), (), s32[]{:S(2)}) async-start(), calls=%async_computation.17 | async-start | bytes 5242880 | tf_op jit(solution)/shard_map/reduce_scatter | solution.py:230
  1237.0 25.5 %collective-permute-start.30 = (bf16[128,4096]{1,0:T(8,128)(2,1)}, bf16[128,4096]{1,0:T(8,128)(2,1)}, u32[]{:S(2)}, u32[]{:S(2)}) collective-permute-start(bf16[128,4096]{1,0:T(8,128)(2,1)} %fusion.225), channel_id=1, source_target_pairs={{0,1},{1,2},{2,3},{3,0},{4,5},{5,6},{6,7},{7,4},{8,9},{9,10},{10,1... | collective-permute-start | bytes 3145736 | tf_op jit(solution)/shard_map/ppermute | solution.py:158
  1237.3 27.2 %collective-permute-start.32 = (bf16[128,4096]{1,0:T(8,128)(2,1)}, bf16[128,4096]{1,0:T(8,128)(2,1)}, u32[]{:S(2)}, u32[]{:S(2)}) collective-permute-start(bf16[128,4096]{1,0:T(8,128)(2,1)} %fusion.225), channel_id=1, source_target_pairs={{1,0},{2,1},{3,2},{0,3},{5,4},{6,5},{7,6},{4,7},{9,8},{10,9},{11,1... | collective-permute-start | bytes 3145736 | tf_op jit(solution)/shard_map/ppermute | solution.py:161
  1262.6 28.6 %collective-permute-start.29 = (s32[512]{0:T(512)S(1)}, s32[512]{0:T(512)S(1)}, u32[]{:S(2)}, u32[]{:S(2)}) collective-permute-start(s32[512]{0:T(512)S(1)} %collective-permute-done.24), channel_id=1, source_target_pairs={{0,32},{32,64},{64,96},{96,0},{1,33},{33,65},{65,97},{97,1},{2,34}... | collective-permute-start | bytes 6152 | tf_op jit(solution)/shard_map/ppermute | solution.py:56
  1390.7 49.5 %collective-permute-start.34 = (bf16[128,4096]{1,0:T(8,128)(2,1)S(1)}, bf16[128,4096]{1,0:T(8,128)(2,1)S(1)}, u32[]{:S(2)}, u32[]{:S(2)}) collective-permute-start(bf16[128,4096]{1,0:T(8,128)(2,1)S(1)} %collective-permute-done.33), channel_id=1, source_target_pairs={{0,32},{32,64},{64,96},{96,0},{1,33},{33,65},{65,97},{97,1},{2,34}... | collective-permute-start | bytes 3145736 | tf_op jit(solution)/shard_map/ppermute | solution.py:56
  (36 other events, 568.0 us)
Sparse Core Ops, SparseCore 0:
  13.2 69.3 all-gather.2
  334.6 72.6 reduce-scatter.7
  522.7 44.2 reduce-scatter.9
  681.9 45.5 reduce-scatter.11
  842.4 45.5 reduce-scatter.13
  1002.9 45.5 reduce-scatter.15
  1135.1 73.8 reduce-scatter.17
  1293.9 70.3 reduce-scatter.19
